TPU v7x, 32 devices: a whole 2x2x4 slice. The times are simulated.
32 devices in a mesh: gz: 8 (over y, x, core), gy: 4 (over z).
Axes of the slice: x: 2, y: 2, z: 4, core: 2. Of those that a mesh axis runs over, the one named last changes fastest.
Arguments:
- source: float32 [128, 256, 256], P(('gz', 'gy')), may hold values from -8 to 8
- vertical: float32 [128], P(('gz', 'gy')), may hold values from 1 to 64
- reaction: float32 [128, 256, 256], P(('gz', 'gy')), may hold values from 0.05 to 2
Outputs:
- solution: float32 [128, 256, 256], P(('gz', 'gy'))
- norms: float32 [2], replicated
All inputs are finite; a program needn't handle non-finite values.
Results may differ from a plain program's by a relative error of at most 0.0001.
Values sent between devices are 32-bit elements; how exact they have to be, the bound alone decides.
A program may use at most 192 MiB of HBM per device.

v0:
```python
import functools

import jax
import jax.numpy as jnp
import numpy as np
from jax import lax
from jax.experimental import pallas as pl
from jax.experimental.pallas import tpu as pltpu
from jax.sharding import PartitionSpec as P

LEVELS = 5
SWITCH = 2
CYCLES = 2
SWEEPS = 2
COARSE = 4
DAMPING = 0.8
COUPLING = 1.0
CHUNK = 32
MESH = pl.DeviceIdType.MESH


def dot(a, b):
    return lax.dot_general(
        a,
        b,
        (((1,), (0,)), ((), ())),
        precision=lax.Precision.HIGHEST,
        preferred_element_type=jnp.float32,
    )


def kernel(
    dims,
    source, reaction, vert_s, vert_b, down0, downt0, down1, cols, mask, group, ups, groupt, colst,
    out, norms,
    v0, v1, w0, d1, w1, g1, r1, tmp0, res1, corr1, send_a, recv_a, send_v, recv_v, recv_b,
    send_n, recv_n, lines, diag, factor, target, around, halo, rowbuf, acc,
    plane_send, plane_recv, line_send, line_recv, a2a_send, a2a_recv,
):
    gz, gy, depth, cp = dims
    nd = gz * gy
    zall = nd * depth
    n0 = source.shape[1]
    n1 = n0 // 2
    a_me = lax.axis_index("gz")
    b_me = lax.axis_index("gy")
    me = a_me * gy + b_me
    h = [COUPLING / 4.0**k for k in range(LEVELS)]

    @pl.when(me == 0)
    def _():
        for p in range(2):
            v0[p, 0] = jnp.zeros((n0, n0), jnp.float32)
            v1[p, 0] = jnp.zeros((n1, n1), jnp.float32)

    @pl.when(me == nd - 1)
    def _():
        for p in range(2):
            v0[p, depth + 1] = jnp.zeros((n0, n0), jnp.float32)
            v1[p, depth + 1] = jnp.zeros((n1, n1), jnp.float32)

    edges = [a_me == 0, a_me == gz - 1, b_me == 0, b_me == gy - 1]
    for k in range(4):
        @pl.when(edges[k])
        def _(k=k):
            for p in range(2):
                halo[p, k] = jnp.zeros((zall, cp), jnp.float32)

    def flat(d):
        return (d // gy, d % gy)

    def plane_copy(v, p, level, up):
        if up:
            src, dst, to = v.at[p, depth], v.at[p, 0], flat(me + 1)
        else:
            src, dst, to = v.at[p, 1], v.at[p, depth + 1], flat(me + nd - 1 - nd * ((me + nd - 1) // nd))
        if up:
            to = flat((me + 1) % nd)
        k = 0 if up else 1
        return pltpu.make_async_remote_copy(
            src_ref=src, dst_ref=dst,
            send_sem=plane_send.at[level, p, k], recv_sem=plane_recv.at[level, p, k],
            device_id=to, device_id_type=MESH,
        )

    def plane_start(v, p, level):
        @pl.when(me < nd - 1)
        def _():
            plane_copy(v, p, level, True).start()

        @pl.when(me > 0)
        def _():
            plane_copy(v, p, level, False).start()

    def plane_wait(v, p, level):
        @pl.when(me < nd - 1)
        def _():
            plane_copy(v, p, level, True).wait_send()
            plane_copy(v, p, level, False).wait_recv()

        @pl.when(me > 0)
        def _():
            plane_copy(v, p, level, False).wait_send()
            plane_copy(v, p, level, True).wait_recv()

    def residual_chunk(v, p, z, r, n, target_ref, diag_of, weight):
        centre = v[p, z, pl.ds(r, CHUNK), :]
        rows = lax.broadcasted_iota(jnp.int32, (CHUNK, n), 0)
        lanes = lax.broadcasted_iota(jnp.int32, (CHUNK, n), 1)
        if r == 0:
            above = jnp.where(rows == 0, 0.0, pltpu.roll(centre, 1, 0))
        else:
            above = v[p, z, pl.ds(r - 1, CHUNK), :]
        if r + CHUNK == n:
            below = jnp.where(rows == CHUNK - 1, 0.0, pltpu.roll(centre, CHUNK - 1, 0))
        else:
            below = v[p, z, pl.ds(r + 1, CHUNK), :]
        left = jnp.where(lanes == 0, 0.0, pltpu.roll(centre, 1, 1))
        right = jnp.where(lanes == n - 1, 0.0, pltpu.roll(centre, n - 1, 1))
        vert = vert_s[z - 1]
        applied = (
            diag_of(z - 1, r, vert) * centre
            - vert * (v[p, z - 1, pl.ds(r, CHUNK), :] + v[p, z + 1, pl.ds(r, CHUNK), :])
            - weight * (above + below + left + right)
        )
        return centre, target_ref[z - 1, pl.ds(r, CHUNK), :] - applied

    def diag0(z, r, vert):
        return 2.0 * vert + 4.0 * h[0] + reaction[z, pl.ds(r, CHUNK), :]

    def diag1(z, r, vert):
        return d1[z, pl.ds(r, CHUNK), :]

    def over_planes(v, p, level, body):
        plane_start(v, p, level)

        def inner(z, c):
            body(z)
            return c

        lax.fori_loop(2, depth, inner, 0)
        plane_wait(v, p, level)

        def outer(i, c):
            body(1 + i * (depth - 1))
            return c

        lax.fori_loop(0, 2, outer, 0)

    def level_parts(level):
        if level == 0:
            return v0, source, diag0, w0, n0
        return v1, g1, diag1, w1, n1

    def sweep(level, p, record=None):
        v, tgt, dg, w, n = level_parts(level)

        def body(z):
            for r in range(0, n, CHUNK):
                centre, res = residual_chunk(v, p, z, r, n, tgt, dg, h[level])
                v[1 - p, z, pl.ds(r, CHUNK), :] = centre + w[z - 1, pl.ds(r, CHUNK), :] * res
                if record is not None:
                    sq = (res * res).reshape(CHUNK // 8, 8, n).sum(axis=0)
                    acc[record, :, :] += sq

        over_planes(v, p, level, body)
        return 1 - p

    def first_sweep(level):
        v, tgt, dg, w, n = level_parts(level)

        def body(z, c):
            v[0, z + 1] = w[z] * tgt[z]
            return c

        lax.fori_loop(0, depth, body, 0)
        return 0

    def restrict0(read_chunk, store):
        def body(z):
            for r in range(0, n0, CHUNK):
                tmp0[pl.ds(r, CHUNK), :] = dot(read_chunk(z, r), downt0[...])
            store(z, dot(down0[...], tmp0[...]))
        return body

    def restrict1(z, plane):
        half = dot(down1[...], plane)
        for b in range(gy):
            spread = dot(half, cols[b]) * mask[...]
            packed = dot(group[...], spread)
            for a in range(gz):
                send_a[b, a, z : z + 1, :] = packed[a : a + 1, :]

    def exchange_all(kind, src_of, recv):
        def copy(k):
            dst = (me + k) % nd
            a, b = dst // gy, dst % gy
            return pltpu.make_async_remote_copy(
                src_ref=src_of(a, b), dst_ref=recv.at[b_me, a_me],
                send_sem=a2a_send.at[kind, k], recv_sem=a2a_recv.at[kind, me],
                device_id=(a, b), device_id_type=MESH,
            )

        def start(k, c):
            copy(k).start()
            return c

        def finish(k, c):
            copy(k).wait_send()
            src = (me + k) % nd
            a, b = src // gy, src % gy
            pltpu.make_async_remote_copy(
                src_ref=recv.at[b, a], dst_ref=recv.at[b, a],
                send_sem=a2a_send.at[kind, k], recv_sem=a2a_recv.at[kind, src],
                device_id=(a, b), device_id_type=MESH,
            ).wait_recv()
            return c

        def begin():
            lax.fori_loop(1, nd, start, 0)

        def end():
            lax.fori_loop(1, nd, finish, 0)

        return begin, end

    def to_lines(recv, dest):
        for a in range(gz):
            for b in range(gy):
                s = (a * gy + b) * depth
                dest[s : s + depth, :] = recv[b, a]

    bx2, by2 = (n1 // 2 // gz, n1 // 2 // gy)
    steps = []
    s = 1
    while s < zall:
        steps.append(s)
        s *= 2
    ns = len(steps)

    def setup_lines(offset):
        rows = lax.broadcasted_iota(jnp.int32, (zall, cp), 0)
        vert = lines[...]
        a = jnp.where(rows == 0, 0.0, -vert)
        c = jnp.where(rows == zall - 1, 0.0, -vert)
        b = diag[offset]
        for k, s in enumerate(steps):
            alpha = -a / pltpu.roll(b, s, 0)
            gamma = -c / pltpu.roll(b, zall - s, 0)
            b = b + alpha * pltpu.roll(c, s, 0) + gamma * pltpu.roll(a, zall - s, 0)
            a = alpha * pltpu.roll(a, s, 0)
            c = gamma * pltpu.roll(c, zall - s, 0)
            factor[offset, 2 * k] = alpha
            factor[offset, 2 * k + 1] = gamma
        factor[offset, 2 * ns] = 1.0 / b

    def solve(offset, right):
        for k, s in enumerate(steps):
            right = (
                right
                + factor[offset, 2 * k] * pltpu.roll(right, s, 0)
                + factor[offset, 2 * k + 1] * pltpu.roll(right, zall - s, 0)
            )
        return right * factor[offset, 2 * ns]

    count = [0]
    def line_copy(p, k):
        if k == 0:
            to, slot = ((a_me + gz - 1) % gz, b_me), 1
        elif k == 1:
            to, slot = ((a_me + 1) % gz, b_me), 0
        elif k == 2:
            to, slot = (a_me, (b_me + gy - 1) % gy), 3
        else:
            to, slot = (a_me, (b_me + 1) % gy), 2
        return pltpu.make_async_remote_copy(
            src_ref=around.at[p], dst_ref=halo.at[p, slot],
            send_sem=line_send.at[p, k], recv_sem=line_recv.at[p, slot],
            device_id=to, device_id_type=MESH,
        )

    def line_landed(p, k):
        return pltpu.make_async_remote_copy(
            src_ref=around.at[p], dst_ref=halo.at[p, k],
            send_sem=line_send.at[p, k], recv_sem=line_recv.at[p, k],
            device_id=(a_me, b_me), device_id_type=MESH,
        )

    def neighbours(offset, values):
        bx, by = bx2 >> offset, by2 >> offset
        cells = bx * by
        p = count[0] % 2
        count[0] += 1
        around[p] = values
        for k in range(4):
            @pl.when(jnp.logical_not(edges[k]))
            def _(k=k):
                line_copy(p, k).start()
        for k in range(4):
            @pl.when(jnp.logical_not(edges[k]))
            def _(k=k):
                line_copy(p, k).wait_send()
                line_landed(p, k).wait_recv()
        lane = lax.broadcasted_iota(jnp.int32, (zall, cp), 1)

        def roll(x, amount):
            amount = amount % cp
            return x if amount == 0 else pltpu.roll(x, amount, 1)

        total = jnp.where(lane < by, roll(halo[p, 0], by - cells), roll(values, by))
        total += jnp.where(lane >= cells - by, roll(halo[p, 1], cells - by), roll(values, -by))
        inrow = lane & (by - 1)
        total += jnp.where(inrow == 0, roll(halo[p, 2], 1 - by), roll(values, 1))
        total += jnp.where(inrow == by - 1, roll(halo[p, 3], by - 1), roll(values, -1))
        return total

    def line_descend(offset):
        weight = h[SWITCH + offset]
        values = solve(offset, target[offset])
        repeats = COARSE if offset == LEVELS - 1 - SWITCH else SWEEPS
        for _ in range(1, repeats):
            values = solve(offset, target[offset] + weight * neighbours(offset, values))
        if offset == LEVELS - 1 - SWITCH:
            return values
        near = neighbours(offset, values)
        rows = lax.broadcasted_iota(jnp.int32, (zall, cp), 0)
        before = jnp.where(rows == 0, 0.0, pltpu.roll(values, 1, 0))
        after = jnp.where(rows == zall - 1, 0.0, pltpu.roll(values, zall - 1, 0))
        res = target[offset] - (
            diag[offset] * values - lines[...] * (before + after) - weight * near
        )
        target[offset + 1] = dot(res, ups[2 * offset])
        tmp = values
        lower = line_descend(offset + 1)
        values = tmp + dot(lower, ups[2 * offset + 1])
        for _ in range(SWEEPS):
            values = solve(offset, target[offset] + weight * neighbours(offset, values))
        return values

    def fill0(z, c):
        w0[z] = DAMPING / (2.0 * vert_s[z] + 4.0 * h[0] + reaction[z])
        return c

    lax.fori_loop(0, depth, fill0, 0)

    def keep_r1(z, value):
        r1[z] = value
        dv = 2.0 * vert_s[z] + 4.0 * h[1] + value
        d1[z] = dv
        w1[z] = DAMPING / dv

    body = restrict0(lambda z, r: reaction[z, pl.ds(r, CHUNK), :], keep_r1)
    lax.fori_loop(0, depth, lambda z, c: (body(z), c)[1], 0)
    for z in range(depth):
        restrict1(z, r1[z])
    send_v[...] = send_a[...]
    begin_v, end_v = exchange_all(0, lambda a, b: vert_b, recv_v)
    begin_r, end_r = exchange_all(1, lambda a, b: send_v.at[b, a], recv_a)
    begin_v()
    begin_r()
    recv_v[b_me, a_me] = vert_b[...]
    recv_a[b_me, a_me] = send_v[b_me, a_me]
    acc[...] = jnp.zeros_like(acc)

    begin_a, end_a = exchange_all(2, lambda a, b: send_a.at[b, a], recv_b.at[0])
    begin_b, end_b = exchange_all(3, lambda a, b: send_n.at[b, a], recv_b.at[1])

    p0 = first_sweep(0)
    for cycle in range(CYCLES):
        for k in range(SWEEPS):
            if cycle == 0 and k == 0:
                continue
            p0 = sweep(0, p0, record=cycle - 1 if cycle > 0 and k == 0 else None)

        def read0(z, r, p0=p0):
            return residual_chunk(v0, p0, z, r, n0, source, diag0, h[0])[1]

        def keep_g1(z, value):
            g1[z - 1] = value

        over_planes(v0, p0, 0, restrict0(read0, keep_g1))
        p1 = first_sweep(1)
        for k in range(1, SWEEPS):
            p1 = sweep(1, p1)

        def keep_res(z, p1=p1):
            for r in range(0, n1, CHUNK):
                res1[z - 1, pl.ds(r, CHUNK), :] = residual_chunk(
                    v1, p1, z, r, n1, g1, diag1, h[1]
                )[1]

        over_planes(v1, p1, 1, keep_res)
        for z in range(depth):
            restrict1(z, res1[z])
        begin_a()
        recv_b[0, b_me, a_me] = send_a[b_me, a_me]
        if cycle == 0:
            end_v()
            end_r()
            to_lines(recv_v, lines)
            to_lines(recv_a, target.at[0])
            coarse = target[0]
            for offset in range(LEVELS - SWITCH):
                if offset > 0:
                    coarse = dot(coarse, ups[2 * offset - 2])
                diag[offset] = 2.0 * lines[...] + 4.0 * h[SWITCH + offset] + coarse
            for offset in range(LEVELS - SWITCH):
                setup_lines(offset)
        end_a()
        to_lines(recv_b.at[0], target.at[0])
        rowbuf[...] = line_descend(0)
        for a in range(gz):
            for b in range(gy):
                s = (a * gy + b) * depth
                send_n[b, a] = rowbuf[s : s + depth, :]
        begin_b()
        recv_b[1, b_me, a_me] = send_n[b_me, a_me]
        end_b()
        for z in range(depth):
            wide = None
            for b in range(gy):
                for a in range(gz):
                    corr1[a : a + 1, :] = recv_b[1, b, a, z : z + 1, :]
                part = dot(dot(groupt[...], corr1[...]) * mask[...], colst[b])
                wide = part if wide is None else wide + part
            v1[1 - p1, z + 1] = v1[p1, z + 1] + dot(down1[...].T * 2.0, wide)
        p1 = 1 - p1
        for _ in range(SWEEPS):
            p1 = sweep(1, p1)

        def correct0(z, c, p0=p0, p1=p1):
            tmp0[...] = dot(down0[...].T * 2.0, v1[p1, z])
            for r in range(0, n0, CHUNK):
                v0[1 - p0, z, pl.ds(r, CHUNK), :] = v0[p0, z, pl.ds(r, CHUNK), :] + dot(
                    tmp0[pl.ds(r, CHUNK), :], downt0[...].T * 2.0
                )
            return c

        lax.fori_loop(1, depth + 1, correct0, 0)
        p0 = 1 - p0
        for _ in range(SWEEPS):
            p0 = sweep(0, p0)

    def last(z, p0=p0):
        for r in range(0, n0, CHUNK):
            centre, res = residual_chunk(v0, p0, z, r, n0, source, diag0, h[0])
            out[z - 1, pl.ds(r, CHUNK), :] = centre
            acc[CYCLES - 1, :, :] += (res * res).reshape(CHUNK // 8, 8, n0).sum(axis=0)

    over_planes(v0, p0, 0, last)
    ridx = lax.broadcasted_iota(jnp.int32, (8, 128), 0)
    part = jnp.zeros((8, 128), jnp.float32)
    for k in range(CYCLES):
        part = jnp.where(ridx == k, jnp.sum(acc[k]), part)
    rowbuf_n = tmp_n = send_n
    target_n = recv_n
    w_n = acc
    acc[0, :, 0:128] = part
    begin_n, end_n = exchange_all(4, lambda a, b: acc.at[0, :, pl.ds(0, 128)], recv_n)
    begin_n()
    recv_n[b_me, a_me] = part
    end_n()
    total = jnp.zeros((8, 128), jnp.float32)
    for a in range(gz):
        for b in range(gy):
            total = total + recv_n[b, a]
    norms[...] = total * (1.0 / (zall * n0 * n0))


def pair_matrix(n, value):
    return (np.arange(n)[None, :] // 2 == np.arange(n // 2)[:, None]).astype(np.float32) * value


def shards(gz, gy, source, vertical, reaction):
    depth, n0 = source.shape[0], source.shape[1]
    nd = gz * gy
    zall = nd * depth
    n1, n2 = n0 // 2, n0 // 4
    bx, by = n2 // gz, n2 // gy
    cells = bx * by
    cp = -(-cells // 128) * 128
    down0 = pair_matrix(n0, 0.5)
    down1 = pair_matrix(n1, 0.5)
    lane = np.arange(cp)
    cols = np.zeros((gy, n1, cp), np.float32)
    colst = np.zeros((gy, cp, n1), np.float32)
    for b in range(gy):
        hit = (np.arange(n1)[:, None] // 2 == b * by + lane[None, :] % by) & (lane[None, :] < cells)
        cols[b] = hit * 0.5
        colst[b] = hit.T
    mask = ((lane[None, :] // by == np.arange(n2)[:, None] % bx) & (lane[None, :] < cells)).astype(np.float32)
    group = (np.arange(n2)[None, :] // bx == np.arange(gz)[:, None]).astype(np.float32)
    ups = []
    for offset in range(LEVELS - SWITCH - 1):
        fx, fy = bx >> offset, by >> offset
        cy = fy // 2
        matrix = np.zeros((cp, cp), np.float32)
        for i in range(fx):
            for j in range(fy):
                matrix[i * fy + j, (i // 2) * cy + j // 2] = 1.0
        ups += [matrix * 0.25, matrix.T]
    ups = np.stack(ups)
    steps = (zall - 1).bit_length()
    f32 = jnp.float32
    nl = LEVELS - SWITCH
    vm = pl.BlockSpec(memory_space=pltpu.VMEM)
    consts = [down0, down0.T.copy(), down1, cols, mask, group, ups, group.T.copy(), colst]
    solution, norms = pl.pallas_call(
        functools.partial(kernel, (gz, gy, depth, cp)),
        out_shape=(
            jax.ShapeDtypeStruct(source.shape, f32),
            jax.ShapeDtypeStruct((8, 128), f32),
        ),
        in_specs=[vm, vm, pl.BlockSpec(memory_space=pltpu.SMEM), vm] + [vm] * len(consts),
        out_specs=(vm, vm),
        scratch_shapes=[
            pltpu.VMEM((2, depth + 2, n0, n0), f32),
            pltpu.VMEM((2, depth + 2, n1, n1), f32),
            pltpu.VMEM((depth, n0, n0), f32),
            pltpu.VMEM((depth, n1, n1), f32),
            pltpu.VMEM((depth, n1, n1), f32),
            pltpu.VMEM((depth, n1, n1), f32),
            pltpu.VMEM((depth, n1, n1), f32),
            pltpu.VMEM((n0, n1), f32),
            pltpu.VMEM((depth, n1, n1), f32),
            pltpu.VMEM((gz, cp), f32),
            pltpu.VMEM((gy, gz, depth, cp), f32),
            pltpu.VMEM((gy, gz, depth, cp), f32),
            pltpu.VMEM((gy, gz, depth, cp), f32),
            pltpu.VMEM((gy, gz, depth, cp), f32),
            pltpu.VMEM((2, gy, gz, depth, cp), f32),
            pltpu.VMEM((gy, gz, depth, cp), f32),
            pltpu.VMEM((gy, gz, 8, 128), f32),
            pltpu.VMEM((zall, cp), f32),
            pltpu.VMEM((nl, zall, cp), f32),
            pltpu.VMEM((nl, 2 * steps + 1, zall, cp), f32),
            pltpu.VMEM((nl, zall, cp), f32),
            pltpu.VMEM((2, zall, cp), f32),
            pltpu.VMEM((2, 4, zall, cp), f32),
            pltpu.VMEM((zall, cp), f32),
            pltpu.VMEM((CYCLES, 8, n0), f32),
            pltpu.SemaphoreType.DMA((2, 2, 2)),
            pltpu.SemaphoreType.DMA((2, 2, 2)),
            pltpu.SemaphoreType.DMA((2, 4)),
            pltpu.SemaphoreType.DMA((2, 4)),
            pltpu.SemaphoreType.DMA((5, nd)),
            pltpu.SemaphoreType.DMA((5, nd)),
        ],
        compiler_params=pltpu.CompilerParams(
            has_side_effects=True, vmem_limit_bytes=64000 * 1024
        ),
    )(
        source,
        reaction,
        vertical,
        jnp.broadcast_to(vertical[:, None], (depth, cp)),
        *[jnp.asarray(c) for c in consts],
    )
    return solution, norms[:CYCLES, 0]


def solution(mesh):
    return jax.shard_map(
        functools.partial(shards, mesh.shape["gz"], mesh.shape["gy"]),
        mesh=mesh,
        in_specs=(P(("gz", "gy"), None, None), P(("gz", "gy")), P(("gz", "gy"), None, None)),
        out_specs=(P(("gz", "gy"), None, None), P()),
        check_vma=False,
    )
```

profile of v0, /device:TPU:0, one launch (start us, length us, event | category | flops | bytes accessed | tf_op | source)
XLA Modules:
  0.0 348.3 jit_solution(5424671115862422347)
XLA Ops:
  0.6 1.3 broadcast_in_dim.2.vert_b
  1.9 342.7 %shard_map.131 = (f32[4,256,256]{2,1,0:T(8,128)}, f32[8,128]{1,0:T(8,128)}) custom-call(f32[4,256,256]{2,1,0:T(8,128)} %source.1, f32[4,256,256]{2,1,0:T(8,128)} %reaction.1, f32[4]{0:T(128)} %vert_s.1, f32[4,128]{1,0:T(4,128)} %broadcast_in_dim.2.vert_b, f32[128,256]{1,0:T(8,128)} %constant.18.clone.down0, f32[256,128]{1,0:T(8,128)} %constant.19.clone.downt0, ...), custom_call_target="tpu_custom_call" | custom-call | tf_op jit(solution)/shard_map/pallas_call | solution.py:508
  344.7 1.3 slice_reduce_fusion
  346.0 2.3 copy.15
where the time goes:
time: 348 us
  Pallas kernels  343 us (99%)
  local copies, waits for them, and re-layouts  4.89 us (1%)
    pallas_call x1, Pallas kernels, shards(): pl.pallas_call(functools.partial(kernel, (gz, gy, depth, cp)), out_shape=...  343 us

commit v1 on v0

--- a/solution.py
+++ b/solution.py
@@ -27,6 +27,32 @@
         precision=lax.Precision.HIGHEST,
         preferred_element_type=jnp.float32,
     )
+
+
+def parts_of(x):
+    first = x.astype(jnp.bfloat16)
+    rest = x - first.astype(jnp.float32)
+    second = rest.astype(jnp.bfloat16)
+    third = (rest - second.astype(jnp.float32)).astype(jnp.bfloat16)
+    return (third, second, first)
+
+
+def dot_right(x, m):
+    m = m.astype(jnp.bfloat16)
+    total = None
+    for x in parts_of(x):
+        term = jnp.dot(x, m, preferred_element_type=jnp.float32)
+        total = term if total is None else total + term
+    return total
+
+
+def dot_left(m, x):
+    m = m.astype(jnp.bfloat16)
+    total = None
+    for x in parts_of(x):
+        term = jnp.dot(m, x, preferred_element_type=jnp.float32)
+        total = term if total is None else total + term
+    return total
 
 
 def kernel(
@@ -179,8 +205,8 @@
     def restrict0(read_chunk, store):
         def body(z):
             for r in range(0, n0, CHUNK):
-                tmp0[pl.ds(r, CHUNK), :] = dot(read_chunk(z, r), downt0[...])
-            store(z, dot(down0[...], tmp0[...]))
+                tmp0[pl.ds(r, CHUNK), :] = dot_right(read_chunk(z, r), downt0[...])
+            store(z, dot_left(down0[...], tmp0[...]))
         return body
 
     def restrict1(z, plane):
@@ -429,10 +455,10 @@
             p1 = sweep(1, p1)
 
         def correct0(z, c, p0=p0, p1=p1):
-            tmp0[...] = dot(down0[...].T * 2.0, v1[p1, z])
+            tmp0[...] = dot_left(downt0[...] * 2.0, v1[p1, z])
             for r in range(0, n0, CHUNK):
-                v0[1 - p0, z, pl.ds(r, CHUNK), :] = v0[p0, z, pl.ds(r, CHUNK), :] + dot(
-                    tmp0[pl.ds(r, CHUNK), :], downt0[...].T * 2.0
+                v0[1 - p0, z, pl.ds(r, CHUNK), :] = v0[p0, z, pl.ds(r, CHUNK), :] + dot_right(
+                    tmp0[pl.ds(r, CHUNK), :], down0[...] * 2.0
                 )
             return c
 

time: 348 us -> 342 us (0.983)
  Pallas kernels: 343 us -> 337 us
    pallas_call x1, Pallas kernels: 343 us -> 337 us  [shards(): pl.pallas_call(functools.partial(kernel, (gz, gy, depth, cp)), out_shape=...]
where the time goes in v1:
time: 342 us
  Pallas kernels  337 us (99%)
  local copies, waits for them, and re-layouts  4.89 us (1%)
    pallas_call x1, Pallas kernels, shards(): pl.pallas_call(functools.partial(kernel, (gz, gy, depth, cp)), out_shape=...  337 us

profile of v1, /device:TPU:0, one launch (start us, length us, event | category | flops | bytes accessed | tf_op | source)
XLA Modules:
  0.0 342.2 jit_solution(14245980939128280456)
XLA Ops:
  0.6 1.3 broadcast_in_dim.2.vert_b
  1.9 336.7 %shard_map.131 = (f32[4,256,256]{2,1,0:T(8,128)}, f32[8,128]{1,0:T(8,128)}) custom-call(f32[4,256,256]{2,1,0:T(8,128)} %source.1, f32[4,256,256]{2,1,0:T(8,128)} %reaction.1, f32[4]{0:T(128)} %vert_s.1, f32[4,128]{1,0:T(4,128)} %broadcast_in_dim.2.vert_b, f32[128,256]{1,0:T(8,128)} %constant.18.clone.down0, f32[256,128]{1,0:T(8,128)} %constant.19.clone.downt0, ...), custom_call_target="tpu_custom_call" | custom-call | tf_op jit(solution)/shard_map/pallas_call | solution.py:534
  338.6 1.3 slice_reduce_fusion
  339.9 2.3 copy.15
